TPU v7x, 32 devices: a whole 2x2x4 slice. The times are simulated.
32 devices in a mesh: inst: 4 (over y, x), scen: 8 (over z, core).
Axes of the slice: x: 2, y: 2, z: 4, core: 2. Of those that a mesh axis runs over, the one named last changes fastest.
Arguments:
- positions: int32 [512, 16384], P(None, 'inst'), may hold values from -50 to 50
- holding_block_grid: int32 [8, 128], P(None, 'inst'), may hold values 0 or 1
- risk: float32 [16384, 8192], P('inst', 'scen'), may hold values from -64 to 64
Outputs:
- margin: float32 [512], P('inst')
- gradient: float32 [512, 16384], P('scen', 'inst')
All inputs are finite; a program needn't handle non-finite values. No bound on the sum of `holding_block_grid` on one device may be relied on, other than what follows from the above.
Results may differ from a plain program's by a relative error of at most 0.0003.
Values sent between devices are 32-bit elements; how exact they have to be, the bound alone decides.
A program may use at most 64 MiB of HBM per device.

v0:
```python
import functools
import math

import jax
import jax.numpy as jnp
from jax import lax
from jax.experimental import pallas as pl
from jax.experimental.pallas import tpu as pltpu
from jax.sharding import PartitionSpec as P

ABLK = 64
IBLK = 128
CORES = 2
LANES = 128
STAGES = 3
PIECE = 1024
STRIP = 16


def chunk_plan(rows, chips, inst_number):
    unit = max(16, 2 * inst_number)
    plan = []
    for phase in range(chips // 2):
        done = 0
        while done < rows:
            small = phase == 0 and done < 2 * unit
            take = min(unit if small else 2 * unit, rows - done)
            plan.append((chips - 1 - phase, phase, done, take))
            done += take
    return plan


def kernel(
    cfg,
    positions,
    grid,
    risk,
    margin_out,
    gradient_out,
    stage,
    pos_buf,
    held,
    high,
    low,
    part,
    rs_buf,
    full,
    tails,
    peaks,
    totals,
    stats,
    factor,
    partial,
    pair_buf,
    line_buf,
    marg,
    stage_sem,
    pos_sem,
    rs_send,
    rs_recv,
    ag_send,
    ag_recv,
    stats_send,
    stats_recv,
    pair_send,
    pair_recv,
    line_send,
    line_recv,
):
    plan, accounts, insts, scens, softness, total_scen = cfg
    instruments, scen_here = risk.shape
    rows = accounts // scens
    chips = scens // CORES
    piece = min(PIECE, instruments)
    pieces = instruments // piece
    kblock = stage.shape[1]
    kblocks = instruments // kblock
    number = len(plan)
    inst = lax.axis_index("inst")
    me = lax.axis_index("scen")
    z = me // CORES
    core = me % CORES
    far = z // (chips // 2)

    sizes = [4 * take for _, _, _, take in plan]
    starts = [sum(sizes[:c]) for c in range(number)]
    head = sizes[0] + sizes[1]

    def owner_of(c, slot):
        above, below, _, _ = plan[c]
        return above - slot * (above - below)

    def load_risk(b):
        slot = b % STAGES
        return pltpu.make_async_copy(
            risk.at[pl.ds(b * kblock, kblock), :], stage.at[slot], stage_sem.at[slot]
        )

    def pos_copies(c, slot, base):
        _, _, first, take = plan[c]
        copies = []
        for s in range(2):
            for k in range(CORES):
                account = (owner_of(c, s) * CORES + k) * rows + first
                group = s * CORES + k
                copies.append(
                    pltpu.make_async_copy(
                        positions.at[pl.ds(account, take), :],
                        pos_buf.at[slot, pl.ds(base + group * take, take), :],
                        pos_sem.at[slot, base // sizes[0] if base else 0, group],
                    )
                )
        return copies

    def make_held(c, slot, base):
        _, _, first, take = plan[c]

        def column(j, carry):
            cols = pl.ds(pl.multiple_of(j * IBLK, IBLK), IBLK)
            for s in range(2):
                for k in range(CORES):
                    account = (owner_of(c, s) * CORES + k) * rows + first
                    live = grid[account // ABLK, j].astype(jnp.float32)
                    lines = pl.ds(base + (s * CORES + k) * take, take)
                    held[lines, cols] = (
                        pos_buf[slot, lines, cols].astype(jnp.float32) * live
                    ).astype(jnp.bfloat16)
            return carry

        lax.fori_loop(0, instruments // IBLK, column, 0)

    for copy in pos_copies(0, 0, 0) + pos_copies(1, 0, sizes[0]):
        copy.start()
    for b in range(min(STAGES, kblocks)):
        load_risk(b).start()
    if number > 2:
        for copy in pos_copies(2, 1, 0):
            copy.start()

    barrier = pltpu.get_barrier_semaphore()
    for i in range(1, insts):
        pl.semaphore_signal(barrier, inc=1, device_id={"inst": (inst + i) % insts})
    for i in range(1, scens):
        pl.semaphore_signal(barrier, inc=1, device_id={"scen": (me + i) % scens})

    peaks[...] = jnp.zeros_like(peaks)
    totals[...] = jnp.ones_like(totals)
    marg[...] = jnp.zeros_like(marg)
    part[pl.ds(0, head), :] = jnp.zeros((head, scen_here), jnp.float32)

    for copy in pos_copies(0, 0, 0) + pos_copies(1, 0, sizes[0]):
        copy.wait()
    make_held(0, 0, 0)
    make_held(1, 0, sizes[0])
    if number > 3:
        for copy in pos_copies(3, 0, 0):
            copy.start()

    def arrive(b, carry):
        slot = b % STAGES
        load_risk(b).wait()

        def split(r, inner):
            lines = pl.ds(pl.multiple_of(r * STRIP, STRIP), STRIP)
            value = stage[slot, lines, :]
            top = value.astype(jnp.bfloat16)
            there = pl.ds(pl.multiple_of(b * kblock + r * STRIP, STRIP), STRIP)
            high[there, :] = top
            low[there, :] = (value - top.astype(jnp.float32)).astype(jnp.bfloat16)
            return inner

        lax.fori_loop(0, kblock // STRIP, split, 0, unroll=2)

        @pl.when(b + STAGES < kblocks)
        def _():
            load_risk(b + STAGES).start()

        deep = pl.ds(pl.multiple_of(b * kblock, kblock), kblock)
        mine = held[pl.ds(0, head), deep]
        part[pl.ds(0, head), :] += jnp.dot(
            mine, high[deep, :], preferred_element_type=jnp.float32
        ) + jnp.dot(mine, low[deep, :], preferred_element_type=jnp.float32)
        return carry

    lax.fori_loop(0, kblocks, arrive, 0)

    def profit(c):
        slot = (c - 1) % 2
        for copy in pos_copies(c, slot, 0):
            copy.wait()
        make_held(c, slot, 0)
        if c + 2 < number:
            for copy in pos_copies(c + 2, slot, 0):
                copy.start()
        width = 256

        def column(n, carry):
            cols = pl.ds(pl.multiple_of(n * width, width), width)
            mine = held[pl.ds(0, sizes[c]), :]
            part[pl.ds(starts[c], sizes[c]), cols] = jnp.dot(
                mine, high[:, cols], preferred_element_type=jnp.float32
            ) + jnp.dot(mine, low[:, cols], preferred_element_type=jnp.float32)
            return carry

        lax.fori_loop(0, scen_here // width, column, 0)

    def rs_copy(c, i):
        group = sizes[c] // insts
        to = (inst + i) % insts
        return pltpu.make_async_remote_copy(
            part.at[pl.ds(pl.multiple_of(starts[c] + to * group, 8), group), :],
            rs_buf.at[i - 1, pl.ds(starts[c] // insts, group), :],
            rs_send.at[c, i - 1],
            rs_recv.at[c, i - 1],
            device_id={"inst": to},
        )

    def ag_copy(c, i, source):
        group = sizes[c] // insts
        lines = pl.ds(pl.multiple_of(starts[c] + source * group, 8), group)
        return pltpu.make_async_remote_copy(
            full.at[lines, :],
            full.at[lines, :],
            ag_send.at[c, i - 1],
            ag_recv.at[c, i - 1],
            device_id={"inst": (inst + i) % insts},
        )

    def send_parts(c):
        for i in range(1, insts):
            rs_copy(c, i).start()

    def sum_and_gather(c):
        group = sizes[c] // insts
        lines = pl.ds(pl.multiple_of(starts[c] + inst * group, 8), group)
        value = part[lines, :]
        for i in range(1, insts):
            rs_copy(c, i).wait_recv()
            value = value + rs_buf[i - 1, pl.ds(starts[c] // insts, group), :]
        full[lines, :] = value
        for i in range(1, insts):
            ag_copy(c, i, inst).start()

    def stats_copy(c, i):
        return pltpu.make_async_remote_copy(
            stats.at[c, 0],
            stats.at[c, i],
            stats_send.at[c, i - 1],
            stats_recv.at[c, i - 1],
            device_id={"scen": (me + i) % scens},
        )

    def weigh(c):
        size = sizes[c]
        for i in range(1, insts):
            ag_copy(c, i, (inst + insts - i) % insts).wait_recv()

        def strip(r, carry):
            lines = pl.ds(pl.multiple_of(r * STRIP, STRIP), STRIP)
            score = full[pl.ds(pl.multiple_of(starts[c] + r * STRIP, STRIP), STRIP), :] * (
                -1.0 / softness
            )
            peak = jnp.max(score, axis=1, keepdims=True)
            tail = jnp.exp(score - peak)
            total = jnp.sum(tail, axis=1, keepdims=True)
            top = tail.astype(jnp.bfloat16)
            tails[lines, :] = top
            tails[pl.ds(pl.multiple_of(size + r * STRIP, STRIP), STRIP), :] = (
                tail - top.astype(jnp.float32)
            ).astype(jnp.bfloat16)
            peaks[lines, :] = jnp.broadcast_to(peak, (STRIP, LANES))
            totals[lines, :] = jnp.broadcast_to(total, (STRIP, LANES))
            return carry

        lax.fori_loop(0, size // STRIP, strip, 0)
        stats[c, 0, 0:1, :] = jnp.transpose(peaks[...])[0:1, :]
        stats[c, 0, 1:2, :] = jnp.transpose(totals[...])[0:1, :]
        for i in range(1, scens):
            stats_copy(c, i).start()

    def multiply(c):
        size = sizes[c]
        width = 512
        over = (((1,), (1,)), ((), ()))

        def column(n, carry):
            cols = pl.ds(pl.multiple_of(n * width, width), width)
            both = lax.dot_general(
                tails[pl.ds(0, 2 * size), :], high[cols, :], over,
                preferred_element_type=jnp.float32,
            )
            rest = lax.dot_general(
                tails[pl.ds(0, size), :], low[cols, :], over,
                preferred_element_type=jnp.float32,
            )
            partial[pl.ds(starts[c], size), cols] = both[:size] + (both[size:] + rest)
            return carry

        lax.fori_loop(0, instruments // width, column, 0)

    def pair_copy(c, slot, p):
        _, _, _, take = plan[c]
        cols = pl.ds(pl.multiple_of(p * piece, piece), piece)
        away = starts[c] + (slot * CORES + (1 - core)) * take
        return pltpu.make_async_remote_copy(
            partial.at[pl.ds(pl.multiple_of(away, 8), take), cols],
            pair_buf.at[pl.ds(pl.multiple_of(starts[c] // 2 + slot * take, 8), take), cols],
            pair_send.at[c, slot, p],
            pair_recv.at[c, slot, p],
            device_id={"scen": z * CORES + (1 - core)},
        )

    def scale_and_pair(c):
        _, _, _, take = plan[c]
        for i in range(1, scens):
            stats_copy(c, i).wait_recv()
        peak = stats[c, 0, 0:1, :]
        for i in range(1, scens):
            peak = jnp.maximum(peak, stats[c, i, 0:1, :])
        total = stats[c, 0, 1:2, :] * jnp.exp(stats[c, 0, 0:1, :] - peak)
        for i in range(1, scens):
            total = total + stats[c, i, 1:2, :] * jnp.exp(stats[c, i, 0:1, :] - peak)
        scale = -jnp.exp(stats[c, 0, 0:1, :] - peak) / total
        factor[...] = jnp.transpose(jnp.broadcast_to(scale, (LANES, LANES)))
        value = jnp.broadcast_to(peak + jnp.log(total) - math.log(total_scen), (8, LANES))
        lane = lax.broadcasted_iota(jnp.int32, (8, LANES), 1)
        for slot in range(2):
            for k in range(CORES):
                account = (owner_of(c, slot) * CORES + k) * rows + plan[c][2]
                line, at = account // LANES, account % LANES
                src = (slot * CORES + k) * take
                moved = pltpu.roll(value, (at - src) % LANES, 1)
                keep = jnp.logical_and(lane >= at, lane < at + take)
                marg[line : line + 1, :] = jnp.where(keep, moved, marg[line : line + 1, :])[0:1, :]

        def column(p, carry):
            cols = pl.ds(pl.multiple_of(p * piece, piece), piece)
            for g in range(4 * take // 8):
                lines = pl.ds(starts[c] + g * 8, 8)
                partial[lines, cols] = partial[lines, cols] * factor[pl.ds(g * 8, 8), 0:1]
            pair_copy(c, far, p).start()
            pair_copy(c, 1 - far, p).start()
            return carry

        lax.fori_loop(0, pieces, column, 0)

    def mine_at(c, slot, p):
        _, _, _, take = plan[c]
        cols = pl.ds(pl.multiple_of(p * piece, piece), piece)
        return pl.ds(pl.multiple_of(starts[c] + (slot * CORES + core) * take, 8), take), cols

    def there_at(c, slot, p):
        _, _, _, take = plan[c]
        cols = pl.ds(pl.multiple_of(p * piece, piece), piece)
        return pl.ds(pl.multiple_of(starts[c] // 2 + slot * take, 8), take), cols

    def line_copy(c, slot, p, way):
        lines, cols = mine_at(c, slot, p)
        there, _ = there_at(c, slot, p)
        return pltpu.make_async_remote_copy(
            partial.at[lines, cols],
            line_buf.at[way, there, cols],
            line_send.at[c, slot, p],
            line_recv.at[way, c, slot, p],
            device_id={"scen": me + CORES if way == 0 else me - CORES},
        )

    def join_pair(c):
        for slot in (far, 1 - far):
            owner = owner_of(c, slot)

            def step(p, carry):
                lines, cols = mine_at(c, slot, p)
                there, _ = there_at(c, slot, p)
                pair_copy(c, slot, p).wait_recv()
                partial[lines, cols] += pair_buf[there, cols]

                @pl.when(jnp.logical_and(z == 0, owner > 0))
                def _():
                    line_copy(c, slot, p, 0).start()

                @pl.when(jnp.logical_and(z == chips - 1, owner < chips - 1))
                def _():
                    line_copy(c, slot, p, 1).start()

                return carry

            lax.fori_loop(0, pieces, step, 0)

    def forward(c):
        for slot in (far, 1 - far):
            owner = owner_of(c, slot)
            up = jnp.logical_and(z > 0, owner > z)
            down = jnp.logical_and(z < chips - 1, owner < z)
            for way, here in ((0, up), (1, down)):

                @pl.when(here)
                def _():
                    def step(p, carry):
                        lines, cols = mine_at(c, slot, p)
                        there, _ = there_at(c, slot, p)
                        copy = line_copy(c, slot, p, way)
                        copy.wait_recv()
                        partial[lines, cols] += line_buf[way, there, cols]
                        copy.start()
                        return carry

                    lax.fori_loop(0, pieces, step, 0)

    def finish(c):
        _, _, first, take = plan[c]
        for slot in range(2):
            owner = owner_of(c, slot)

            @pl.when(z == owner)
            def _():
                def step(p, carry):
                    lines, cols = mine_at(c, slot, p)
                    there, _ = there_at(c, slot, p)
                    if owner == 0:
                        line_copy(c, slot, p, 1).wait_recv()
                        value = partial[lines, cols] + line_buf[1, there, cols]
                    elif owner == chips - 1:
                        line_copy(c, slot, p, 0).wait_recv()
                        value = partial[lines, cols] + line_buf[0, there, cols]
                    else:
                        line_copy(c, slot, p, 0).wait_recv()
                        value = partial[lines, cols] + line_buf[0, there, cols]
                        line_copy(c, slot, p, 1).wait_recv()
                        value = value + line_buf[1, there, cols]
                    gradient_out[pl.ds(first, take), cols] = value
                    return carry

                lax.fori_loop(0, pieces, step, 0)

    pl.semaphore_wait(barrier, insts - 1 + scens - 1)
    send_parts(0)
    sum_and_gather(0)
    send_parts(1)
    if number > 2:
        profit(2)
    for c in range(number):
        weigh(c)
        multiply(c)
        if c + 1 < number:
            sum_and_gather(c + 1)
        scale_and_pair(c)
        if c == 0 and number > 2:
            send_parts(2)
        join_pair(c)
        if c > 0:
            forward(c - 1)
            if c + 2 < number:
                profit(c + 2)
                send_parts(c + 2)
    for c in range(number - 1):
        finish(c)
    forward(number - 1)
    finish(number - 1)

    share = accounts // insts
    if share % LANES == 0:
        margin_out[...] = marg[pl.ds(inst * (share // LANES), share // LANES), :]
    else:
        margin_out[...] = marg[pl.ds(inst * share // LANES, 1), :]

    for c in range(number):
        for i in range(1, insts):
            rs_copy(c, i).wait_send()
            ag_copy(c, i, inst).wait_send()
        for i in range(1, scens):
            stats_copy(c, i).wait_send()
        for slot in range(2):
            owner = owner_of(c, slot)

            def drain(p, carry):
                pair_copy(c, slot, p).wait_send()

                @pl.when(owner > z)
                def _():
                    line_copy(c, slot, p, 0).wait_send()

                @pl.when(owner < z)
                def _():
                    line_copy(c, slot, p, 1).wait_send()

                return carry

            lax.fori_loop(0, pieces, drain, 0)


def body(positions, holding_block_grid, risk):
    accounts, instruments = positions.shape
    scen_here = risk.shape[1]
    insts = lax.axis_size("inst")
    scens = lax.axis_size("scen")
    chips = scens // CORES
    rows = accounts // scens
    softness = 8.0 * math.sqrt(instruments * insts)
    plan = chunk_plan(rows, chips, insts)
    number = len(plan)
    share = accounts // insts
    most = max(4 * take for _, _, _, take in plan)
    head = 4 * (plan[0][3] + plan[1][3])
    pieces = instruments // min(PIECE, instruments)
    kblock = min(512, instruments)
    cfg = (plan, accounts, insts, scens, softness, scen_here * scens)
    dma = pltpu.SemaphoreType.DMA
    margin, gradient = pl.pallas_call(
        functools.partial(kernel, cfg),
        out_shape=(
            jax.ShapeDtypeStruct((max(1, share // LANES), LANES), jnp.float32),
            jax.ShapeDtypeStruct((rows, instruments), jnp.float32),
        ),
        in_specs=[
            pl.BlockSpec(memory_space=pl.ANY),
            pl.BlockSpec(memory_space=pltpu.SMEM),
            pl.BlockSpec(memory_space=pl.ANY),
        ],
        out_specs=(
            pl.BlockSpec(memory_space=pltpu.VMEM),
            pl.BlockSpec(memory_space=pltpu.VMEM),
        ),
        scratch_shapes=[
            pltpu.VMEM((STAGES, kblock, scen_here), jnp.float32),
            pltpu.VMEM((2, max(most, head), instruments), jnp.int32),
            pltpu.VMEM((max(most, head), instruments), jnp.bfloat16),
            pltpu.VMEM((instruments, scen_here), jnp.bfloat16),
            pltpu.VMEM((instruments, scen_here), jnp.bfloat16),
            pltpu.VMEM((accounts, scen_here), jnp.float32),
            pltpu.VMEM((insts - 1, accounts // insts, scen_here), jnp.float32),
            pltpu.VMEM((accounts, scen_here), jnp.float32),
            pltpu.VMEM((2 * most, scen_here), jnp.bfloat16),
            pltpu.VMEM((LANES, LANES), jnp.float32),
            pltpu.VMEM((LANES, LANES), jnp.float32),
            pltpu.VMEM((number, scens, 2, LANES), jnp.float32),
            pltpu.VMEM((LANES, LANES), jnp.float32),
            pltpu.VMEM((accounts, instruments), jnp.float32),
            pltpu.VMEM((accounts // 2, instruments), jnp.float32),
            pltpu.VMEM((2, accounts // 2, instruments), jnp.float32),
            pltpu.VMEM((max(8, accounts // LANES), LANES), jnp.float32),
            dma((STAGES,)),
            dma((2, 2, 4)),
            dma((number, insts - 1)),
            dma((number, insts - 1)),
            dma((number, insts - 1)),
            dma((number, insts - 1)),
            dma((number, scens - 1)),
            dma((number, scens - 1)),
            dma((number, 2, pieces)),
            dma((number, 2, pieces)),
            dma((number, 2, pieces)),
            dma((2, number, 2, pieces)),
        ],
        compiler_params=pltpu.CompilerParams(
            collective_id=0, has_side_effects=True, vmem_limit_bytes=67043328
        ),
    )(positions, holding_block_grid, risk)
    if share % LANES == 0:
        margin = margin.reshape(share)
    else:
        start = (lax.axis_index("inst") * share) % LANES
        margin = lax.dynamic_slice_in_dim(margin.reshape(LANES), start, share)
    return (margin, gradient)


def solution(mesh):
    placed = (P(None, "inst"), P(None, "inst"), P("inst", "scen"))
    return jax.shard_map(
        body, mesh=mesh, in_specs=placed, out_specs=(P("inst"), P("scen", "inst")), check_vma=False
    )
```

profile of v0, /device:TPU:8, one launch (start us, length us, event | category | flops | bytes accessed | tf_op | source)
XLA Modules:
  0.0 144.3 jit_solution(3659012671204097932)
XLA Ops:
  0.6 140.3 %shard_map.50 = (f32[1,128]{1,0:T(1,128)}, f32[64,4096]{1,0:T(8,128)}) custom-call(s32[512,4096]{1,0:T(8,128)} %positions.1, s32[8,32]{1,0:T(8,128)} %grid.1, f32[4096,1024]{1,0:T(8,128)} %risk.1), custom_call_target="tpu_custom_call" | custom-call | tf_op jit(solution)/shard_map/pallas_call | solution.py:509
  140.9 1.1 copy.7
  142.0 2.3 %copy.8 = f32[64,4096]{1,0:T(8,128)} copy(f32[64,4096]{1,0:T(8,128)} %get-tuple-element.9) | data formatting | bytes 2097152
where the time goes:
time: 145 us; the launch traced here: 144 us
  Pallas kernels  140 us (97%)
  local copies, waits for them, and re-layouts  3.38 us (2%)
    pallas_call x1, Pallas kernels, body(): pl.pallas_call(functools.partial(kernel, cfg), out_shape=(jax.ShapeDtypeS...  140 us
    unnamed x2, local copies, waits for them, and re-layouts  3.38 us

commit v1 on v0

--- a/solution.py
+++ b/solution.py
@@ -19,15 +19,15 @@
 
 def chunk_plan(rows, chips, inst_number):
     unit = max(16, 2 * inst_number)
-    plan = []
+    inner, outer = [], []
     for phase in range(chips // 2):
         done = 0
+        last = phase == chips // 2 - 1
         while done < rows:
-            small = phase == 0 and done < 2 * unit
-            take = min(unit if small else 2 * unit, rows - done)
-            plan.append((chips - 1 - phase, phase, done, take))
+            take = min(unit if last and done < 2 * unit else 2 * unit, rows - done)
+            (inner if last else outer).append((chips - 1 - phase, phase, done, take))
             done += take
-    return plan
+    return inner[:2] + outer + inner[2:]
 
 
 def kernel(
@@ -50,6 +50,7 @@
     totals,
     stats,
     factor,
+    line_factor,
     partial,
     pair_buf,
     line_buf,
@@ -112,7 +113,7 @@
                 )
         return copies
 
-    def make_held(c, slot, base):
+    def make_held(c, slot, base, shift=0):
         _, _, first, take = plan[c]
 
         def column(j, carry):
@@ -122,7 +123,7 @@
                     account = (owner_of(c, s) * CORES + k) * rows + first
                     live = grid[account // ABLK, j].astype(jnp.float32)
                     lines = pl.ds(base + (s * CORES + k) * take, take)
-                    held[lines, cols] = (
+                    held[pl.ds(shift + base + (s * CORES + k) * take, take), cols] = (
                         pos_buf[slot, lines, cols].astype(jnp.float32) * live
                     ).astype(jnp.bfloat16)
             return carry
@@ -184,25 +185,29 @@
 
     lax.fori_loop(0, kblocks, arrive, 0)
 
-    def profit(c):
+    width = min(256, scen_here)
+    blocks = scen_here // width
+    shifted = pos_buf.shape[1]
+
+    def profit_load(c):
         slot = (c - 1) % 2
         for copy in pos_copies(c, slot, 0):
             copy.wait()
-        make_held(c, slot, 0)
+        make_held(c, slot, 0, c % 2 * shifted)
         if c + 2 < number:
             for copy in pos_copies(c + 2, slot, 0):
                 copy.start()
-        width = 256
-
+
+    def profit(c, begin, end):
         def column(n, carry):
             cols = pl.ds(pl.multiple_of(n * width, width), width)
-            mine = held[pl.ds(0, sizes[c]), :]
+            mine = held[pl.ds(c % 2 * shifted, sizes[c]), :]
             part[pl.ds(starts[c], sizes[c]), cols] = jnp.dot(
                 mine, high[:, cols], preferred_element_type=jnp.float32
             ) + jnp.dot(mine, low[:, cols], preferred_element_type=jnp.float32)
             return carry
 
-        lax.fori_loop(0, scen_here // width, column, 0)
+        lax.fori_loop(begin, end, column, 0)
 
     def rs_copy(c, i):
         group = sizes[c] // insts
@@ -278,26 +283,6 @@
         for i in range(1, scens):
             stats_copy(c, i).start()
 
-    def multiply(c):
-        size = sizes[c]
-        width = 512
-        over = (((1,), (1,)), ((), ()))
-
-        def column(n, carry):
-            cols = pl.ds(pl.multiple_of(n * width, width), width)
-            both = lax.dot_general(
-                tails[pl.ds(0, 2 * size), :], high[cols, :], over,
-                preferred_element_type=jnp.float32,
-            )
-            rest = lax.dot_general(
-                tails[pl.ds(0, size), :], low[cols, :], over,
-                preferred_element_type=jnp.float32,
-            )
-            partial[pl.ds(starts[c], size), cols] = both[:size] + (both[size:] + rest)
-            return carry
-
-        lax.fori_loop(0, instruments // width, column, 0)
-
     def pair_copy(c, slot, p):
         _, _, _, take = plan[c]
         cols = pl.ds(pl.multiple_of(p * piece, piece), piece)
@@ -310,39 +295,96 @@
             device_id={"scen": z * CORES + (1 - core)},
         )
 
-    def scale_and_pair(c):
-        _, _, _, take = plan[c]
+    peer = 1 + (1 - core) * (scens - 2)
+
+    def columns_of(values):
+        line = lax.broadcasted_iota(jnp.int32, (LANES, LANES), 0)
+        table = jnp.zeros((LANES, LANES), jnp.float32)
+        for n, value in enumerate(values):
+            table = jnp.where(line == n, jnp.broadcast_to(value, (LANES, LANES)), table)
+        return jnp.transpose(table)
+
+    def pair_factors(c):
+        stats_copy(c, peer).wait_recv()
+        mine = stats[c, 0, 0:1, :]
+        other = stats[c, peer, 0:1, :]
+        both = jnp.maximum(mine, other)
+        factor[...] = columns_of([-jnp.exp(mine - both), -jnp.exp(other - both)])
+
+    def multiply(c, begin, end):
+        size = sizes[c]
+        over = (((1,), (1,)), ((), ()))
+
+        def column(p, carry):
+            @pl.when(p < pieces)
+            def _():
+                cols = pl.ds(pl.multiple_of(p * piece, piece), piece)
+                both = lax.dot_general(
+                    tails[pl.ds(0, 2 * size), :], high[cols, :], over,
+                    preferred_element_type=jnp.float32,
+                )
+                rest = lax.dot_general(
+                    tails[pl.ds(0, size), :], low[cols, :], over,
+                    preferred_element_type=jnp.float32,
+                )
+                partial[pl.ds(starts[c], size), cols] = both[:size] + (both[size:] + rest)
+                pair_copy(c, far, p).start()
+                pair_copy(c, 1 - far, p).start()
+
+            @pl.when(p == 1)
+            def _():
+                pair_factors(c)
+
+            @pl.when(p > 0)
+            def _():
+                join_pair(c, p - 1)
+
+            return carry
+
+        lax.fori_loop(begin, end, column, 0)
+
+    def settle(c):
+        _, _, first, take = plan[c]
         for i in range(1, scens):
-            stats_copy(c, i).wait_recv()
-        peak = stats[c, 0, 0:1, :]
-        for i in range(1, scens):
-            peak = jnp.maximum(peak, stats[c, i, 0:1, :])
-        total = stats[c, 0, 1:2, :] * jnp.exp(stats[c, 0, 0:1, :] - peak)
-        for i in range(1, scens):
+
+            @pl.when(peer != i)
+            def _():
+                stats_copy(c, i).wait_recv()
+
+        lowest = jnp.full((1, LANES), -3e38, jnp.float32)
+        below, here, above = lowest, lowest, lowest
+        for i in range(scens):
+            chip = ((me + scens - i) % scens) // CORES
+            value = stats[c, i, 0:1, :]
+            below = jnp.maximum(below, jnp.where(chip < z, value, lowest))
+            here = jnp.maximum(here, jnp.where(chip == z, value, lowest))
+            above = jnp.maximum(above, jnp.where(chip > z, value, lowest))
+        peak = jnp.maximum(jnp.maximum(below, above), here)
+        total = jnp.zeros((1, LANES), jnp.float32)
+        for i in range(scens):
             total = total + stats[c, i, 1:2, :] * jnp.exp(stats[c, i, 0:1, :] - peak)
-        scale = -jnp.exp(stats[c, 0, 0:1, :] - peak) / total
-        factor[...] = jnp.transpose(jnp.broadcast_to(scale, (LANES, LANES)))
+        up, down = jnp.maximum(below, here), jnp.maximum(above, here)
+        line_factor[c] = columns_of(
+            [
+                jnp.exp(here - up),
+                jnp.exp(below - up),
+                jnp.exp(here - down),
+                jnp.exp(above - down),
+                jnp.exp(here - peak) / total,
+                jnp.exp(below - peak) / total,
+                jnp.exp(above - peak) / total,
+            ]
+        )
         value = jnp.broadcast_to(peak + jnp.log(total) - math.log(total_scen), (8, LANES))
         lane = lax.broadcasted_iota(jnp.int32, (8, LANES), 1)
         for slot in range(2):
             for k in range(CORES):
-                account = (owner_of(c, slot) * CORES + k) * rows + plan[c][2]
+                account = (owner_of(c, slot) * CORES + k) * rows + first
                 line, at = account // LANES, account % LANES
                 src = (slot * CORES + k) * take
                 moved = pltpu.roll(value, (at - src) % LANES, 1)
                 keep = jnp.logical_and(lane >= at, lane < at + take)
                 marg[line : line + 1, :] = jnp.where(keep, moved, marg[line : line + 1, :])[0:1, :]
-
-        def column(p, carry):
-            cols = pl.ds(pl.multiple_of(p * piece, piece), piece)
-            for g in range(4 * take // 8):
-                lines = pl.ds(starts[c] + g * 8, 8)
-                partial[lines, cols] = partial[lines, cols] * factor[pl.ds(g * 8, 8), 0:1]
-            pair_copy(c, far, p).start()
-            pair_copy(c, 1 - far, p).start()
-            return carry
-
-        lax.fori_loop(0, pieces, column, 0)
 
     def mine_at(c, slot, p):
         _, _, _, take = plan[c]
@@ -365,47 +407,54 @@
             device_id={"scen": me + CORES if way == 0 else me - CORES},
         )
 
-    def join_pair(c):
+    def own_factor(c, slot, n):
+        _, _, _, take = plan[c]
+        lines = pl.ds(pl.multiple_of((slot * CORES + core) * take, 8), take)
+        return line_factor[c, lines, n : n + 1]
+
+    def join_pair(c, p):
+        _, _, _, take = plan[c]
         for slot in (far, 1 - far):
             owner = owner_of(c, slot)
-
-            def step(p, carry):
-                lines, cols = mine_at(c, slot, p)
-                there, _ = there_at(c, slot, p)
-                pair_copy(c, slot, p).wait_recv()
-                partial[lines, cols] += pair_buf[there, cols]
-
-                @pl.when(jnp.logical_and(z == 0, owner > 0))
-                def _():
-                    line_copy(c, slot, p, 0).start()
-
-                @pl.when(jnp.logical_and(z == chips - 1, owner < chips - 1))
-                def _():
-                    line_copy(c, slot, p, 1).start()
-
-                return carry
-
-            lax.fori_loop(0, pieces, step, 0)
-
-    def forward(c):
-        for slot in (far, 1 - far):
-            owner = owner_of(c, slot)
-            up = jnp.logical_and(z > 0, owner > z)
-            down = jnp.logical_and(z < chips - 1, owner < z)
-            for way, here in ((0, up), (1, down)):
-
-                @pl.when(here)
-                def _():
-                    def step(p, carry):
-                        lines, cols = mine_at(c, slot, p)
-                        there, _ = there_at(c, slot, p)
-                        copy = line_copy(c, slot, p, way)
-                        copy.wait_recv()
-                        partial[lines, cols] += line_buf[way, there, cols]
-                        copy.start()
-                        return carry
-
-                    lax.fori_loop(0, pieces, step, 0)
+            lines, cols = mine_at(c, slot, p)
+            there, _ = there_at(c, slot, p)
+            these = pl.ds(pl.multiple_of((slot * CORES + core) * take, 8), take)
+            pair_copy(c, slot, p).wait_recv()
+            partial[lines, cols] = (
+                partial[lines, cols] * factor[these, 0:1] + pair_buf[there, cols] * factor[these, 1:2]
+            )
+
+            @pl.when(jnp.logical_and(z == 0, owner > 0))
+            def _():
+                line_copy(c, slot, p, 0).start()
+
+            @pl.when(jnp.logical_and(z == chips - 1, owner < chips - 1))
+            def _():
+                line_copy(c, slot, p, 1).start()
+
+    def forward(c, order):
+        slot = far if order == 0 else 1 - far
+        if order == 0:
+            settle(c)
+        owner = owner_of(c, slot)
+        up = jnp.logical_and(z > 0, owner > z)
+        down = jnp.logical_and(z < chips - 1, owner < z)
+        for way, here in ((0, up), (1, down)):
+
+            @pl.when(here)
+            def _():
+                def step(p, carry):
+                    lines, cols = mine_at(c, slot, p)
+                    there, _ = there_at(c, slot, p)
+                    copy = line_copy(c, slot, p, way)
+                    copy.wait_recv()
+                    partial[lines, cols] = partial[lines, cols] * own_factor(
+                        c, slot, 2 * way
+                    ) + line_buf[way, there, cols] * own_factor(c, slot, 2 * way + 1)
+                    copy.start()
+                    return carry
+
+                lax.fori_loop(0, pieces, step, 0)
 
     def finish(c):
         _, _, first, take = plan[c]
@@ -417,17 +466,11 @@
                 def step(p, carry):
                     lines, cols = mine_at(c, slot, p)
                     there, _ = there_at(c, slot, p)
-                    if owner == 0:
-                        line_copy(c, slot, p, 1).wait_recv()
-                        value = partial[lines, cols] + line_buf[1, there, cols]
-                    elif owner == chips - 1:
-                        line_copy(c, slot, p, 0).wait_recv()
-                        value = partial[lines, cols] + line_buf[0, there, cols]
-                    else:
-                        line_copy(c, slot, p, 0).wait_recv()
-                        value = partial[lines, cols] + line_buf[0, there, cols]
-                        line_copy(c, slot, p, 1).wait_recv()
-                        value = value + line_buf[1, there, cols]
+                    value = partial[lines, cols] * own_factor(c, slot, 4)
+                    for way in range(2):
+                        if (way == 0 and owner > 0) or (way == 1 and owner < chips - 1):
+                            line_copy(c, slot, p, way).wait_recv()
+                            value = value + line_buf[way, there, cols] * own_factor(c, slot, 5 + way)
                     gradient_out[pl.ds(first, take), cols] = value
                     return carry
 
@@ -435,27 +478,51 @@
 
     pl.semaphore_wait(barrier, insts - 1 + scens - 1)
     send_parts(0)
-    sum_and_gather(0)
     send_parts(1)
     if number > 2:
-        profit(2)
+        profit_load(2)
+        profit(2, 0, blocks)
+    if number > 4:
+        profit_load(4)
+        profit(4, 0, blocks // 2)
+    sum_and_gather(0)
+    if number > 2:
+        send_parts(2)
+    if number > 3:
+        profit_load(3)
+        profit(3, 0, blocks)
+    if number > 4:
+        profit(4, blocks // 2, blocks)
+    sum_and_gather(1)
+    if number > 3:
+        send_parts(3)
+    half = (pieces + 1) // 2
     for c in range(number):
         weigh(c)
-        multiply(c)
-        if c + 1 < number:
-            sum_and_gather(c + 1)
-        scale_and_pair(c)
-        if c == 0 and number > 2:
-            send_parts(2)
-        join_pair(c)
-        if c > 0:
-            forward(c - 1)
-            if c + 2 < number:
-                profit(c + 2)
-                send_parts(c + 2)
-    for c in range(number - 1):
+        multiply(c, 0, half)
+        if c + 2 < number:
+            sum_and_gather(c + 2)
+        if c + 4 < number:
+            send_parts(c + 4)
+        if c >= 4:
+            forward(c - 2, 1)
+        multiply(c, half, pieces + 1)
+        if c + 5 < number:
+            profit_load(c + 5)
+            profit(c + 5, 0, blocks)
+        if c == 2:
+            for n in (0, 1):
+                forward(n, 0)
+                forward(n, 1)
+        if c >= 3:
+            forward(c - 1, 0)
+    if number >= 4:
+        forward(number - 2, 1)
+    for c in range(number - 2):
         finish(c)
-    forward(number - 1)
+    forward(number - 1, 0)
+    forward(number - 1, 1)
+    finish(number - 2)
     finish(number - 1)
 
     share = accounts // insts
@@ -524,7 +591,7 @@
         scratch_shapes=[
             pltpu.VMEM((STAGES, kblock, scen_here), jnp.float32),
             pltpu.VMEM((2, max(most, head), instruments), jnp.int32),
-            pltpu.VMEM((max(most, head), instruments), jnp.bfloat16),
+            pltpu.VMEM((2 * max(most, head), instruments), jnp.bfloat16),
             pltpu.VMEM((instruments, scen_here), jnp.bfloat16),
             pltpu.VMEM((instruments, scen_here), jnp.bfloat16),
             pltpu.VMEM((accounts, scen_here), jnp.float32),
@@ -535,6 +602,7 @@
             pltpu.VMEM((LANES, LANES), jnp.float32),
             pltpu.VMEM((number, scens, 2, LANES), jnp.float32),
             pltpu.VMEM((LANES, LANES), jnp.float32),
+            pltpu.VMEM((number, LANES, LANES), jnp.float32),
             pltpu.VMEM((accounts, instruments), jnp.float32),
             pltpu.VMEM((accounts // 2, instruments), jnp.float32),
             pltpu.VMEM((2, accounts // 2, instruments), jnp.float32),

time: 145 us -> 119 us (0.82)
  Pallas kernels: 140 us -> 115 us
    pallas_call x1, Pallas kernels: 140 us -> 115 us  [body(): pl.pallas_call(functools.partial(kernel, cfg), out_shape=(jax.ShapeDtypeS...]
where the time goes in v1:
time: 119 us
  Pallas kernels  115 us (97%)
  local copies, waits for them, and re-layouts  3.38 us (3%)
    pallas_call x1, Pallas kernels, body(): pl.pallas_call(functools.partial(kernel, cfg), out_shape=(jax.ShapeDtypeS...  115 us
    unnamed x2, local copies, waits for them, and re-layouts  3.38 us

profile of v1, /device:TPU:8, one launch (start us, length us, event | category | flops | bytes accessed | tf_op | source)
XLA Modules:
  0.0 118.5 jit_solution(13261978186450539782)
XLA Ops:
  0.6 114.5 %shard_map.50 = (f32[1,128]{1,0:T(1,128)}, f32[64,4096]{1,0:T(8,128)}) custom-call(s32[512,4096]{1,0:T(8,128)} %positions.1, s32[8,32]{1,0:T(8,128)} %grid.1, f32[4096,1024]{1,0:T(8,128)} %risk.1), custom_call_target="tpu_custom_call" | custom-call | tf_op jit(solution)/shard_map/pallas_call | solution.py:576
  115.2 1.1 copy.7
  116.3 2.3 %copy.8 = f32[64,4096]{1,0:T(8,128)} copy(f32[64,4096]{1,0:T(8,128)} %get-tuple-element.9) | data formatting | bytes 2097152

commit v2 on v1

--- a/solution.py
+++ b/solution.py
@@ -15,6 +15,7 @@
 STAGES = 3
 PIECE = 1024
 STRIP = 16
+SPLIT = 64
 
 
 def chunk_plan(rows, chips, inst_number):
@@ -162,15 +163,15 @@
         load_risk(b).wait()
 
         def split(r, inner):
-            lines = pl.ds(pl.multiple_of(r * STRIP, STRIP), STRIP)
+            lines = pl.ds(pl.multiple_of(r * SPLIT, SPLIT), SPLIT)
             value = stage[slot, lines, :]
             top = value.astype(jnp.bfloat16)
-            there = pl.ds(pl.multiple_of(b * kblock + r * STRIP, STRIP), STRIP)
+            there = pl.ds(pl.multiple_of(b * kblock + r * SPLIT, SPLIT), SPLIT)
             high[there, :] = top
             low[there, :] = (value - top.astype(jnp.float32)).astype(jnp.bfloat16)
             return inner
 
-        lax.fori_loop(0, kblock // STRIP, split, 0, unroll=2)
+        lax.fori_loop(0, kblock // SPLIT, split, 0, unroll=2)
 
         @pl.when(b + STAGES < kblocks)
         def _():
@@ -277,7 +278,7 @@
             totals[lines, :] = jnp.broadcast_to(total, (STRIP, LANES))
             return carry
 
-        lax.fori_loop(0, size // STRIP, strip, 0)
+        lax.fori_loop(0, size // STRIP, strip, 0, unroll=2)
         stats[c, 0, 0:1, :] = jnp.transpose(peaks[...])[0:1, :]
         stats[c, 0, 1:2, :] = jnp.transpose(totals[...])[0:1, :]
         for i in range(1, scens):
@@ -432,10 +433,8 @@
             def _():
                 line_copy(c, slot, p, 1).start()
 
-    def forward(c, order):
+    def forward(c, order, begin, end):
         slot = far if order == 0 else 1 - far
-        if order == 0:
-            settle(c)
         owner = owner_of(c, slot)
         up = jnp.logical_and(z > 0, owner > z)
         down = jnp.logical_and(z < chips - 1, owner < z)
@@ -454,7 +453,7 @@
                     copy.start()
                     return carry
 
-                lax.fori_loop(0, pieces, step, 0)
+                lax.fori_loop(begin, end, step, 0)
 
     def finish(c):
         _, _, first, take = plan[c]
@@ -497,6 +496,7 @@
     if number > 3:
         send_parts(3)
     half = (pieces + 1) // 2
+    cut = pieces // 2
     for c in range(number):
         weigh(c)
         multiply(c, 0, half)
@@ -504,24 +504,36 @@
             sum_and_gather(c + 2)
         if c + 4 < number:
             send_parts(c + 4)
+        if c >= 3:
+            settle(c - 1)
+            forward(c - 1, 0, 0, cut)
         if c >= 4:
-            forward(c - 2, 1)
+            forward(c - 2, 1, 0, cut)
         multiply(c, half, pieces + 1)
         if c + 5 < number:
             profit_load(c + 5)
             profit(c + 5, 0, blocks)
         if c == 2:
             for n in (0, 1):
-                forward(n, 0)
-                forward(n, 1)
+                settle(n)
+                forward(n, 0, 0, pieces)
+                forward(n, 1, 0, pieces)
+        if c >= 4:
+            forward(c - 2, 1, cut, pieces)
         if c >= 3:
-            forward(c - 1, 0)
-    if number >= 4:
-        forward(number - 2, 1)
+            forward(c - 1, 0, cut, pieces)
+    settle(number - 1)
     for c in range(number - 2):
         finish(c)
-    forward(number - 1, 0)
-    forward(number - 1, 1)
+
+    def both(p, carry):
+        if number >= 4:
+            forward(number - 2, 1, p, p + 1)
+        forward(number - 1, 0, p, p + 1)
+        return carry
+
+    lax.fori_loop(0, pieces, both, 0)
+    forward(number - 1, 1, 0, pieces)
     finish(number - 2)
     finish(number - 1)
 

time: 119 us -> 109 us (0.916)
  Pallas kernels: 115 us -> 105 us
    pallas_call x1, Pallas kernels: 115 us -> 105 us  [body(): pl.pallas_call(functools.partial(kernel, cfg), out_shape=(jax.ShapeDtypeS...]
where the time goes in v2:
time: 109 us
  Pallas kernels  105 us (96%)
  local copies, waits for them, and re-layouts  3.38 us (3%)
    pallas_call x1, Pallas kernels, body(): pl.pallas_call(functools.partial(kernel, cfg), out_shape=(jax.ShapeDtypeS...  105 us
    unnamed x2, local copies, waits for them, and re-layouts  3.38 us

profile of v2, /device:TPU:8, one launch (start us, length us, event | category | flops | bytes accessed | tf_op | source)
XLA Modules:
  0.0 108.8 jit_solution(1900372876030167700)
XLA Ops:
  0.6 104.8 %shard_map.50 = (f32[1,128]{1,0:T(1,128)}, f32[64,4096]{1,0:T(8,128)}) custom-call(s32[512,4096]{1,0:T(8,128)} %positions.1, s32[8,32]{1,0:T(8,128)} %grid.1, f32[4096,1024]{1,0:T(8,128)} %risk.1), custom_call_target="tpu_custom_call" | custom-call | tf_op jit(solution)/shard_map/pallas_call | solution.py:588
  105.4 1.1 %copy.7 = f32[128]{0:T(128)} copy(f32[128]{0:T(128)} %bitcast.1) | data formatting | bytes 1024
  106.5 2.3 %copy.8 = f32[64,4096]{1,0:T(8,128)} copy(f32[64,4096]{1,0:T(8,128)} %get-tuple-element.9) | data formatting | bytes 2097152
